TPU v7x, 32 devices: a whole 2x2x4 slice. The times are simulated.
32 devices in a mesh: dp: 8 (over z, y), expert: 4 (over x, core).
Axes of the slice: x: 2, y: 2, z: 4, core: 2. Of those that a mesh axis runs over, the one named last changes fastest.
Arguments:
- queries: bfloat16 [4096, 4096], P('dp', 'expert'), may hold values from -6 to 6
- key_states: bfloat16 [4096, 4096], P('dp', 'expert'), may hold values from -6 to 6
- value_states: bfloat16 [4096, 4096], P('dp', 'expert'), may hold values from -6 to 6
- doc_lengths: int32 [8, 8], replicated, may hold values from 0 to 512, as said below
- move_plan: int32 [8, 2], replicated, may hold values from 0 to 7, as said below
- expert_ids: int32 [4096, 8], P('dp'), may hold values from 0 to 15, all different within a row; in each aligned block of 512 rows (0 to 511, 512 to 1023, ...) at most 384 rows name the same one
- gate_weights: float32 [4096, 8], P('dp'), may hold values from 0.05 to 0.5
- expert_weight: bfloat16 [16, 4096, 1024], P('expert'), may hold values from -0.29882812 to 0.29882812
Outputs:
- attended: bfloat16 [4096, 4096], P('dp', 'expert')
- combined: bfloat16 [4096, 1024], P('dp', 'expert')
- row_load: float32 [8], P('dp')
Inputs may be any that keep to these rules, and one draw needn't show every extreme that they name: `doc_lengths`: each row's entries are the lengths of its packed documents in order and sum to 512; a zero marks an absent document; some row holds a single document. move_plan[r, 0] is r itself or the row half the dp axis away, (r + 8 / 2) mod 8; a row is handed to its partner only if its pairs in all exceed the partner's, so two partners never both move; move_plan[r, 1] is a block number below 2; at least one row moves a block. `expert_ids`: each token names 8 different experts; among the 512 tokens of one row no expert is named by more than 384 tokens.
All inputs are finite; a program needn't handle non-finite values.
Results may differ from a plain program's by a relative error of at most 0.0095.
Values may be sent and summed in bfloat16 or wider, within the bound.
A program may use at most 128 MiB of HBM per device.

v0:
```python
import jax
import jax.numpy as jnp
from jax import lax
from jax.sharding import PartitionSpec as P

HEAD_DIM = 128
QBLOCK = 128
BLOCKS = 4
EXPERTS = 16
CAP = 384


def token_starts(row_lengths, row_count):
    bounds = jnp.cumsum(row_lengths)
    positions = jnp.arange(row_count, dtype=jnp.int32)
    return jnp.max(jnp.where(bounds[None, :] <= positions[:, None], bounds[None, :], 0), axis=1)


def block_pairs(row_lengths, row_count):
    positions = jnp.arange(row_count, dtype=jnp.int32)
    reach = positions - token_starts(row_lengths, row_count) + 1
    return reach.reshape(BLOCKS, QBLOCK).sum(axis=1)


def attend(query_rows, key_rows, value_rows, query_positions, query_starts):
    query_count = query_rows.shape[0]
    key_count = key_rows.shape[0]
    head_count = query_rows.shape[1] // HEAD_DIM
    query_heads = query_rows.reshape(query_count, head_count, HEAD_DIM)
    key_heads = key_rows.reshape(key_count, head_count, HEAD_DIM)
    value_heads = value_rows.reshape(key_count, head_count, HEAD_DIM)
    scores = jnp.einsum(
        "qhd,khd->hqk", query_heads, key_heads, preferred_element_type=jnp.float32
    ) * HEAD_DIM ** (-0.5)
    key_positions = jnp.arange(key_count, dtype=jnp.int32)
    allowed = (key_positions[None, :] <= query_positions[:, None]) & (
        key_positions[None, :] >= query_starts[:, None]
    )
    scores = jnp.where(allowed[None], scores, -jnp.inf)
    weights = jax.nn.softmax(scores, axis=-1).astype(jnp.bfloat16)
    output = jnp.einsum("hqk,khd->qhd", weights, value_heads, preferred_element_type=jnp.float32)
    return output.reshape(query_count, head_count * HEAD_DIM).astype(jnp.bfloat16)


def shards(
    queries,
    key_states,
    value_states,
    doc_lengths,
    move_plan,
    expert_ids,
    gate_weights,
    expert_weight,
):
    dp_size = lax.axis_size("dp")
    group_size = lax.axis_size("expert")
    own_row = lax.axis_index("dp")
    partner = (own_row + dp_size // 2) % dp_size
    row_count = queries.shape[0]
    positions = jnp.arange(row_count, dtype=jnp.int32)
    own_lengths = lax.dynamic_index_in_dim(doc_lengths, own_row, 0, keepdims=False)
    partner_lengths = lax.dynamic_index_in_dim(doc_lengths, partner, 0, keepdims=False)
    own_starts = token_starts(own_lengths, row_count)
    own_plan = lax.dynamic_index_in_dim(move_plan, own_row, 0, keepdims=False)
    partner_plan = lax.dynamic_index_in_dim(move_plan, partner, 0, keepdims=False)
    moving = own_plan[0] != own_row
    incoming = partner_plan[0] != partner
    own_block = own_plan[1]
    their_block = partner_plan[1]

    def run_block(block_index):
        low_row = block_index * QBLOCK
        high_row = low_row + QBLOCK
        return attend(
            queries[low_row:high_row],
            key_states[:high_row],
            value_states[:high_row],
            positions[low_row:high_row],
            own_starts[low_row:high_row],
        )

    attended = jnp.concatenate([run_block(block_index) for block_index in range(BLOCKS)], 0)
    own_pairs = block_pairs(own_lengths, row_count)
    partner_pairs = block_pairs(partner_lengths, row_count)
    row_work = (
        jnp.sum(own_pairs)
        - jnp.where(moving, own_pairs[own_block], 0)
        + jnp.where(incoming, partner_pairs[their_block], 0)
    )
    row_load = (row_work.astype(jnp.float32) / (QBLOCK * QBLOCK)).reshape(1)
    local_experts = EXPERTS // group_size
    expert_range = jnp.arange(EXPERTS, dtype=jnp.int32)
    matches = expert_ids[:, :, None] == expert_range[None, None, :]
    member = jnp.any(matches, axis=1)
    gate_table = jnp.sum(jnp.where(matches, gate_weights[:, :, None], 0.0), axis=1)
    earlier = (positions[None, :] < positions[:, None]).astype(jnp.bfloat16)
    slot_counts = jnp.dot(earlier, member.astype(jnp.bfloat16), preferred_element_type=jnp.float32)
    slot_of = slot_counts.astype(jnp.int32)
    slot_range = jnp.arange(CAP, dtype=jnp.int32)
    dispatch_hot = member.T[:, None, :] & (slot_of.T[:, None, :] == slot_range[None, :, None])
    filled = jnp.any(dispatch_hot, axis=2)
    source = jnp.sum(jnp.where(dispatch_hot, positions[None, None, :], 0), axis=2) + jnp.where(
        filled, 0, row_count
    )
    source = source.reshape(-1)
    member_index = lax.axis_index("expert")
    chosen_rows = lax.dynamic_slice_in_dim(
        source, member_index * local_experts * CAP, local_experts * CAP, 0
    )
    piece = lax.all_gather(attended, "expert", axis=1, tiled=True)
    extended = jnp.concatenate([piece, jnp.zeros((1, piece.shape[1]), piece.dtype)], 0)
    picked = extended[chosen_rows].reshape(local_experts, CAP, piece.shape[1])
    summed = jnp.einsum("ecf,efg->ecg", picked, expert_weight, preferred_element_type=jnp.float32)
    activated = jax.nn.silu(summed).astype(jnp.bfloat16)[None]
    spread = lax.all_to_all(activated, "expert", split_axis=3, concat_axis=0, tiled=True)
    outputs_table = spread.reshape(EXPERTS, CAP, spread.shape[3])
    selected = jnp.einsum(
        "ect,ecg->teg",
        dispatch_hot.astype(jnp.bfloat16),
        outputs_table,
        preferred_element_type=jnp.float32,
    )
    combined = jnp.sum(selected * gate_table[:, :, None], axis=1).astype(jnp.bfloat16)
    return (attended, combined, row_load)


def solution(mesh):
    in_specs = (
        P("dp", "expert"),
        P("dp", "expert"),
        P("dp", "expert"),
        P(),
        P(),
        P("dp", None),
        P("dp", None),
        P("expert", None, None),
    )
    out_specs = (P("dp", "expert"), P("dp", "expert"), P("dp"))
    return jax.shard_map(shards, mesh=mesh, in_specs=in_specs, out_specs=out_specs, check_vma=False)
```

profile of v0, /device:TPU:0, one launch (start us, length us, event | category | flops | bytes accessed | tf_op | source)
XLA Modules:
  0.0 178.1 jit_solution(11677466727423004778)
XLA Ops:
  7.2 0.8 fusion.53
  8.3 1.3 fusion.57
  10.3 1.6 multiply_select_fusion.2
  11.8 0.8 fusion.64
  13.5 0.6 fusion.65
  14.7 1.3 copy.115
  16.0 1.2 copy.95
  17.2 4.2 %convolution_convert_fusion.2 = bf16[8,128,128]{1,2,0:T(8,128)(2,1)S(1)} fusion(bf16[384,8,128]{0,2,1:T(8,128)(2,1)} %bitcast.113, f32[8,128]{1,0:T(8,128)S(1)} %fusion.64, f32[8,128,384]{2,1,0:T(8,128)} %multiply_select_fusion.2), kind=kOutput, calls=%fused_computation.34 | convolution fusion | flops 101975424 | bytes 2625536 | tf_op jit(solution)/shard_map/hqk,khd->qhd/dot_general | solution.py:41
  21.4 0.9 copy.102
  22.5 1.9 %convolution_convert_fusion.3 = bf16[8,128,128]{1,2,0:T(8,128)(2,1)S(1)} fusion(bf16[256,8,128]{0,2,1:T(8,128)(2,1)S(1)} %bitcast.114, f32[8,128]{1,0:T(8,128)S(1)} %fusion.65, f32[8,128,256]{2,1,0:T(8,128)S(1)} %fusion.19), kind=kOutput, calls=%fused_computation.35 | convolution fusion | flops 68027648 | bytes 1839104 | tf_op jit(solution)/shard_map/hqk,khd->qhd/dot_general | solution.py:41
  26.4 2.3 %fusion.61 = (f32[8,128]{1,0:T(8,128)S(1)}, f32[8,128,512]{2,1,0:T(8,128)}) fusion(pred[128,512]{1,0:T(8,128)(4,1)S(1)} %fusion.32, bf16[128,8,128]{0,2,1:T(8,128)(2,1)S(1)} %bitcast.115, bf16[512,1024]{1,0:T(8,128)(2,1)S(1)} %copy-done.1), kind=kOutput, calls=%fused_computation.98 | convolution fusion | flops 136315392 | bytes 3477504 | tf_op jit(solution)/shard_map/sub | solution.py:40
  28.7 2.2 %convolution_convert_fusion = bf16[8,128,128]{1,2,0:T(8,128)(2,1)S(1)} fusion(bf16[512,8,128]{0,2,1:T(8,128)(2,1)S(1)} %bitcast.108, f32[8,128,512]{2,1,0:T(8,128)} %get-tuple-element.26, f32[8,128]{1,0:T(8,128)S(1)} %get-tuple-element.25), kind=kOutput, calls=%fused_computation.32 | convolution fusion | flops 135397376 | bytes 3411968 | tf_op jit(solution)/shard_map/hqk,khd->qhd/dot_general | solution.py:41
  31.1 1.0 pad_maximum_fusion
  32.4 2.1 %fusion.7 = pred[16,384]{1,0:T(8,128)(4,1)S(1)} fusion(s32[16,512]{1,0:T(8,128)S(1)} %convolution_convert_fusion.4, pred[16,512]{1,0:T(8,128)(4,1)S(1)} %bitcast.121), kind=kLoop, calls=%fused_computation.9 | loop fusion | flops 9431040 | bytes 47104 | tf_op jit(solution)/shard_map/reduce_or | solution.py:101
  34.5 2.8 %select_reduce_fusion = s32[16,384]{1,0:T(8,128)S(1)} fusion(s32[16,512]{1,0:T(8,128)S(1)} %convolution_convert_fusion.4, pred[16,512]{1,0:T(8,128)(4,1)S(1)} %bitcast.122), kind=kLoop, calls=%fused_computation.5 | loop fusion | flops 12576768 | bytes 65536 | tf_op jit(solution)/shard_map/reduce_sum | solution.py:102
  37.4 32.1 %all-gather.2.cloned.1.call-done = bf16[512,4096]{1,0:T(8,128)(2,1)} async-done(((bf16[512,1024]{1,0:T(8,128)(2,1)}), bf16[512,4096]{1,0:T(8,128)(2,1)}) %all-gather.2.cloned.1.call-update) | async-done | bytes 4194320 | tf_op jit(solution)/shard_map/all_gather | solution.py:110
  69.5 4.7 %concatenate.7 = bf16[513,4096]{1,0:T(8,128)(2,1)} pad(bf16[512,4096]{1,0:T(8,128)(2,1)} %all-gather.2.cloned.1.call-done, bf16[]{:T(256)} %constant.66.clone.1), padding=0_1x0_0 | pad | bytes 8396802 | tf_op jit(solution)/shard_map/concatenate | solution.py:111
  74.2 25.0 %gather_fusion = bf16[1536,4096]{1,0:T(8,128)(2,1)} fusion(bf16[513,4096]{1,0:T(8,128)(2,1)} %concatenate.7, s32[2048]{0:T(1024)S(1)} %pad_clamp_fusion), kind=kCustom, calls=%fused_computation | custom fusion | bytes 25171968 | tf_op jit(solution)/shard_map/gather | solution.py:112
  99.2 21.3 %fusion.11 = bf16[1,4,384,1024]{3,2,1,0:T(8,128)(2,1)S(1)} fusion(bf16[4,384,4096]{2,1,0:T(8,128)(2,1)} %bitcast.99, bf16[4,4096,1024]{2,1,0:T(8,128)(2,1)} %param.15), kind=kOutput, calls=%fused_computation.15 | convolution fusion | flops 12892766208 | bytes 49283072 | tf_op jit(solution)/shard_map/ecf,efg->ecg/dot_general | solution.py:113
  120.5 3.8 %copy.104 = bf16[1,4,384,1024]{2,1,0,3:T(4,128)(2,1)} copy(bf16[1,4,384,1024]{3,2,1,0:T(8,128)(2,1)S(1)} %fusion.11) | data formatting | bytes 6291456 | tf_op jit(solution)/shard_map/broadcast_in_dim | solution.py:114
  124.3 4.1 %all-to-all-start = ((bf16[1,4,384,1024]{2,1,0,3:T(4,128)(2,1)}), bf16[1,4,384,1024]{2,1,0,3:T(4,128)(2,1)S(1)}, u32[]{:S(2)}, u32[]{:S(2)}) async-start(bf16[1,4,384,1024]{2,1,0,3:T(4,128)(2,1)} %copy.104), calls=%async_computation | async-start | bytes 6291456 | tf_op jit(solution)/shard_map/all_to_all | solution.py:115
  138.3 26.6 %all-to-all-done = bf16[1,4,384,1024]{2,1,0,3:T(4,128)(2,1)S(1)} async-done(((bf16[1,4,384,1024]{2,1,0,3:T(4,128)(2,1)}), bf16[1,4,384,1024]{2,1,0,3:T(4,128)(2,1)S(1)}, u32[]{:S(2)}, u32[]{:S(2)}) %all-to-all-start) | async-done | bytes 3145760 | tf_op jit(solution)/shard_map/all_to_all | solution.py:115
  165.5 3.8 %fusion.8 = bf16[512,256]{0,1:T(8,128)(2,1)S(1)} fusion(f32[512,16]{0,1:T(8,128)S(1)} %select_reduce_fusion.1, bf16[16,384,256]{1,2,0:T(8,128)(2,1)S(1)} %bitcast.101, s32[16,512]{1,0:T(8,128)S(1)} %convolution_convert_fusion.4, pred[16,512]{1,0:T(8,128)(4,1)S(1)} %bitcast.123), kind=kOutput, calls=%fused_computation.11 | convolution fusion | flops 1620967424 | bytes 3481600 | tf_op jit(solution)/shard_map/ect,ecg->teg/dot_general | solution.py:117
  169.3 0.8 copy.106
  (76 shorter events, 8.5 us)
Async XLA Ops:
  7.2 2.6 %slice-start.3 = ((bf16[512,1024]{1,0:T(8,128)(2,1)}), bf16[384,1024]{1,0:T(8,128)(2,1)S(1)}, s32[]{:S(2)}) async-start(bf16[512,1024]{1,0:T(8,128)(2,1)} %param.9), calls=%async_computation.5 | async-start | bytes 1572864 | tf_op jit(solution)/shard_map/slice | solution.py:76
  7.2 62.3 %all-gather.2.cloned.1.call-start = ((), (), s32[]{:S(2)}) async-start(), calls=%async_computation.1 | async-start | bytes 5242880 | tf_op jit(solution)/shard_map/all_gather | solution.py:110
  10.2 2.5 %slice-start.4 = ((bf16[512,1024]{1,0:T(8,128)(2,1)}), bf16[256,1024]{1,0:T(8,128)(2,1)S(1)}, s32[]{:S(2)}) async-start(bf16[512,1024]{1,0:T(8,128)(2,1)} %param.9), calls=%async_computation.6 | async-start | bytes 1048576 | tf_op jit(solution)/shard_map/slice | solution.py:76
  13.5 1.2 copy-start
  14.1 1.9 %slice-start = ((bf16[512,1024]{1,0:T(8,128)(2,1)}), bf16[384,1024]{1,0:T(8,128)(2,1)S(1)}, s32[]{:S(2)}) async-start(bf16[512,1024]{1,0:T(8,128)(2,1)} %param.10), calls=%async_computation.2 | async-start | bytes 1572864 | tf_op jit(solution)/shard_map/slice | solution.py:77
  17.2 5.0 %slice-start.1 = ((bf16[512,1024]{1,0:T(8,128)(2,1)}), bf16[256,1024]{1,0:T(8,128)(2,1)S(1)}, s32[]{:S(2)}) async-start(bf16[512,1024]{1,0:T(8,128)(2,1)} %param.10), calls=%async_computation.3 | async-start | bytes 1048576 | tf_op jit(solution)/shard_map/slice | solution.py:77
  22.4 2.3 %slice-start.5 = ((bf16[512,1024]{1,0:T(8,128)(2,1)}), bf16[128,1024]{1,0:T(8,128)(2,1)S(1)}, s32[]{:S(2)}) async-start(bf16[512,1024]{1,0:T(8,128)(2,1)} %param.9), calls=%async_computation.7 | async-start | bytes 524288 | tf_op jit(solution)/shard_map/slice | solution.py:76
  22.4 3.0 %slice-start.2 = ((bf16[512,1024]{1,0:T(8,128)(2,1)}), bf16[128,1024]{1,0:T(8,128)(2,1)S(1)}, s32[]{:S(2)}) async-start(bf16[512,1024]{1,0:T(8,128)(2,1)} %param.10), calls=%async_computation.4 | async-start | bytes 524288 | tf_op jit(solution)/shard_map/slice | solution.py:77
  24.8 1.6 copy-start.1
  25.9 2.8 %copy-start.2 = (bf16[512,1024]{0,1:T(8,128)(2,1)S(1)}, bf16[512,1024]{0,1:T(8,128)(2,1)}, u32[]{:S(2)}) copy-start(bf16[512,1024]{0,1:T(8,128)(2,1)} %copy.115) | copy-start | bytes 3145732
  28.7 2.3 %copy-start.3 = (bf16[128,1024]{1,0:T(8,128)(2,1)S(1)}, bf16[128,1024]{1,0:T(8,128)(2,1)}, u32[]{:S(2)}) copy-start(bf16[128,1024]{1,0:T(8,128)(2,1)} %copy.102) | copy-start | bytes 786436
  30.9 1.2 copy-start.4
  124.3 4.1 %copy-start.6 = (s32[8,2]{0,1:T(2,128)S(1)}, s32[8,2]{0,1:T(2,128)}, u32[]{:S(2)}) copy-start(s32[8,2]{0,1:T(2,128)} %param.12) | copy-start | bytes 196
  124.3 14.0 %copy-start.5 = (f32[512,8]{0,1:T(8,128)S(1)}, f32[512,8]{0,1:T(8,128)}, u32[]{:S(2)}) copy-start(f32[512,8]{0,1:T(8,128)} %param.14) | copy-start | bytes 49156
  124.3 40.7 %all-to-all-start = ((bf16[1,4,384,1024]{2,1,0,3:T(4,128)(2,1)}), bf16[1,4,384,1024]{2,1,0,3:T(4,128)(2,1)S(1)}, u32[]{:S(2)}, u32[]{:S(2)}) async-start(bf16[1,4,384,1024]{2,1,0,3:T(4,128)(2,1)} %copy.104), calls=%async_computation | async-start | bytes 6291456 | tf_op jit(solution)/shard_map/all_to_all | solution.py:115
Sparse Core Ops, SparseCore 0:
  32.2 37.1 all-gather.1
where the time goes:
time: 179 us; the launch traced here: 178 us
  waiting for transfers between devices  58.7 us (33%)
  local copies, waits for them, and re-layouts  44.9 us (25%)
  matrix products  39.8 us (22%)
  between operations  22.6 us (13%)
  other arithmetic  7.99 us (4%)
  starting transfers between devices  4.13 us (2%)
    all_gather x1, waiting for transfers between devices, shards(): piece = lax.all_gather(attended, 'expert', axis=1, tiled=True)  32.1 us
    all_to_all x1, waiting for transfers between devices, shards(): lax.all_to_all(activated, 'expert', split_axis=3, concat_axis=0, tiled=True)  26.6 us
    gather x1, local copies, waits for them, and re-layouts, shards(): picked = extended[chosen_rows].reshape(local_experts, CAP, piece.shape[1])  25 us
    dot_general x1, matrix products, shards(): jnp.einsum('ecf,efg->ecg', picked, expert_weight, preferred_element_type=...  21.3 us
    dot_general x4, matrix products, attend(): jnp.einsum('hqk,khd->qhd', weights, value_heads, preferred_element_type=j...  8.57 us
    concatenate x1, local copies, waits for them, and re-layouts, shards(): jnp.concatenate([piece, jnp.zeros((1, piece.shape[1]), piece.dtype)], 0)  4.7 us
    all_to_all x1, starting transfers between devices, shards(): lax.all_to_all(activated, 'expert', split_axis=3, concat_axis=0, tiled=True)  4.09 us
    broadcast_in_dim x1, local copies, waits for them, and re-layouts, shards(): activated = jax.nn.silu(summed).astype(jnp.bfloat16)[None]  3.76 us
  transfers between devices with their start and end apart: 2, of which 2 were waited for; matrix products, arithmetic and copies ran while one was open for 5% of the time, Pallas kernels for 0%

commit v1 on v0

v1 whole, which is shorter than its diff:
```python
import functools

import jax
import jax.numpy as jnp
from jax import lax
from jax.experimental import pallas as pl
from jax.experimental.pallas import tpu as pltpu
from jax.sharding import PartitionSpec as P

HEAD_DIM = 128
QBLOCK = 128
MESH = pl.DeviceIdType.MESH
LOG2E = 1.4426950408889634


def span_pairs(low, high, start, stop):
    first = jnp.maximum(low, start)
    last = jnp.minimum(high, stop)
    count = jnp.maximum(last - first, 0)
    return (count * ((first - start + 1) + (last - start))) // 2


def row_pairs(lens, row, block, docs, row_count):
    low = block * QBLOCK
    total = jnp.int32(0)
    picked = jnp.int32(0)
    edge = jnp.int32(0)
    for doc in range(docs):
        stop = edge + lens[row, doc]
        total = total + span_pairs(0, row_count, edge, stop)
        picked = picked + span_pairs(low, low + QBLOCK, edge, stop)
        edge = stop
    return total, picked


def kernel(dp_size, group, q_hbm, k_hbm, v_hbm, lens, plan, ids, gates, w_hbm,
           att_hbm, comb, load,
           qv, kv, vv, wv, xg, acc, bias, gsc, part, rxd, txx, rxx,
           in_sem, w_sem, out_sem,
           sx_sem, rx_sem, sd_sem, rd_sem, sf_sem, rf_sem,
           ps_sem, pr_sem, qs_sem, qr_sem):
    rows, width = q_hbm.shape
    experts, depth, ff = w_hbm.shape
    chips = group // 2
    ck = qv.shape[1] // att_chunks(width)
    chunks = width // ck
    chip_width = 2 * width
    step_width = 2 * ck
    owned = ff // group
    row = lax.axis_index("dp")
    me = lax.axis_index("expert")
    chip = me // 2
    core = lax.rem(me, 2)
    other = chip * 2 + 1 - core

    def in_copies(c):
        cols = pl.ds(pl.multiple_of(c * ck, 128), ck)
        return [
            pltpu.make_async_copy(src.at[:, cols], dst.at[:, cols], in_sem.at[i, c])
            for i, (src, dst) in enumerate(((q_hbm, qv), (k_hbm, kv), (v_hbm, vv)))
        ]

    def place(s, c, k):
        return pl.multiple_of(s * chip_width + c * step_width + k * ck, 128)

    def w_copy(e, s, c, k):
        src = pl.multiple_of((s * 2 + k) * width + c * ck, 128)
        return pltpu.make_async_copy(
            w_hbm.at[e, pl.ds(src, ck), :], wv.at[e, pl.ds(place(s, c, k), ck), :],
            w_sem.at[e, s, c, k])

    def w_start(e, s, c):
        for k in range(2):
            w_copy(e, s, c, k).start()

    def w_wait(e, s, c):
        for k in range(2):
            w_copy(e, s, c, k).wait()

    for c in range(chunks):
        for copy in in_copies(c):
            copy.start()

    barrier = pltpu.get_barrier_semaphore()
    pl.semaphore_signal(barrier, inc=1, device_id={"expert": other}, device_id_type=MESH)
    for d in range(1, chips):
        peer = lax.rem(chip + d, chips) * 2 + core
        pl.semaphore_signal(barrier, inc=1, device_id={"expert": peer}, device_id_type=MESH)

    def start_own(i, _):
        w_start(i // chunks, chip, lax.rem(i, chunks))
        return 0

    lax.fori_loop(0, experts * chunks, start_own, 0)
    for d in range(1, chips):
        def start_far(i, _, d=d):
            w_start(lax.rem(i, experts), lax.rem(chip - d + chips, chips), i // experts)
            return 0

        lax.fori_loop(0, experts * chunks, start_far, 0)

    partner = lax.rem(row + dp_size // 2, dp_size)
    docs = lens.shape[1]
    own_total, own_moved = row_pairs(lens, row, plan[row, 1], docs, rows)
    _, their_moved = row_pairs(lens, partner, plan[partner, 1], docs, rows)
    work = own_total - jnp.where(plan[row, 0] != row, own_moved, 0)
    work = work + jnp.where(plan[partner, 0] != partner, their_moved, 0)
    load[0] = work.astype(jnp.float32) * (1.0 / (QBLOCK * QBLOCK))

    pos = lax.broadcasted_iota(jnp.int32, (rows, rows), 0)
    key_pos = lax.broadcasted_iota(jnp.int32, (rows, rows), 1)
    column = lax.broadcasted_iota(jnp.int32, (rows, 1), 0)
    starts = jnp.zeros((rows, 1), jnp.int32)
    edge = jnp.int32(0)
    for doc in range(docs):
        edge = edge + lens[row, doc]
        starts = jnp.where(column >= edge, jnp.maximum(starts, edge), starts)
    bias[...] = jnp.where((key_pos <= pos) & (key_pos >= starts), 0.0, -1e30)
    for e in range(experts):
        chosen = ids[...] == me * experts + e
        gsc[e] = jnp.sum(jnp.where(chosen, gates[...], 0.0), axis=1, keepdims=True)

    pl.semaphore_wait(barrier, chips)

    def cross_copy(c, d):
        cols = pl.ds(place(chip, c, core), ck)
        return pltpu.make_async_remote_copy(
            src_ref=xg.at[:, cols], dst_ref=xg.at[:, cols],
            send_sem=sx_sem.at[d - 1, c], recv_sem=rx_sem.at[d - 1, c],
            device_id={"expert": lax.rem(chip + d, chips) * 2 + core}, device_id_type=MESH)

    def side_copy(c):
        cols = pl.ds(place(chip, c, core), ck)
        return pltpu.make_async_remote_copy(
            src_ref=xg.at[:, cols], dst_ref=xg.at[:, cols],
            send_sem=sd_sem.at[c], recv_sem=rd_sem.at[c],
            device_id={"expert": other}, device_id_type=MESH)

    def pass_copy(c, d):
        cols = pl.ds(place(lax.rem(chip - d + chips, chips), c, core), ck)
        return pltpu.make_async_remote_copy(
            src_ref=xg.at[:, cols], dst_ref=xg.at[:, cols],
            send_sem=sf_sem.at[d - 1, c], recv_sem=rf_sem.at[d - 1, c],
            device_id={"expert": other}, device_id_type=MESH)

    def out_copy(c):
        return pltpu.make_async_copy(
            xg.at[:, pl.ds(place(chip, c, core), ck)],
            att_hbm.at[:, pl.ds(pl.multiple_of(c * ck, 128), ck)], out_sem.at[c])

    scale = HEAD_DIM ** -0.5 * LOG2E
    qb = rows // 2

    def attend(c, _):
        for copy in in_copies(c):
            copy.wait()
        for h in range(ck // HEAD_DIM):
            cols = pl.ds(pl.multiple_of(c * ck + h * HEAD_DIM, 128), HEAD_DIM)
            dst = pl.ds(pl.multiple_of(place(chip, c, core) + h * HEAD_DIM, 128), HEAD_DIM)
            for b in range(2):
                low, high = b * qb, (b + 1) * qb
                s = lax.dot_general(
                    qv[low:high, cols], kv[:high, cols], (((1,), (1,)), ((), ())),
                    preferred_element_type=jnp.float32)
                s = s + bias[low:high, :high]
                top = jnp.max(s, axis=1, keepdims=True)
                p = jnp.exp2((s - top) * scale)
                norm = jnp.sum(p, axis=1, keepdims=True)
                o = jnp.dot(p.astype(jnp.bfloat16), vv[:high, cols],
                            preferred_element_type=jnp.float32)
                xg[low:high, dst] = (o / norm).astype(jnp.bfloat16)
        for d in range(1, chips):
            cross_copy(c, d).start()
        side_copy(c).start()
        out_copy(c).start()
        return 0

    lax.fori_loop(0, chunks, attend, 0)

    forwards = [(c, d) for c in range(chunks) for d in range(1, chips)]
    sent = [0]

    def forward(count):
        while sent[0] < min(count, len(forwards)):
            c, d = forwards[sent[0]]
            cross_copy(c, d).wait_recv()
            pass_copy(c, d).start()
            sent[0] += 1

    for c in range(chunks):
        side_copy(c).wait_recv()
    own = pl.ds(pl.multiple_of(chip * chip_width, 128), chip_width)
    tile = ff // 2
    for e in range(experts):
        def wait_own(c, _, e=e):
            w_wait(e, chip, c)
            return 0

        lax.fori_loop(0, chunks, wait_own, 0)

        def near(t, _, e=e):
            cols = pl.ds(pl.multiple_of(t * tile, 128), tile)
            acc[e, :, cols] = jnp.dot(xg[:, own], wv[e, own, cols],
                                      preferred_element_type=jnp.float32)
            return 0

        lax.fori_loop(0, 2, near, 0)
        if e == 0 or e == experts - 2:
            forward(sent[0] + 1)

    for i, (c, d) in enumerate(forwards):
        last = i == len(forwards) - 1
        forward(i + 2 if i + 2 < len(forwards) else i + 1)
        src = lax.rem(chip - d + chips, chips)
        pass_copy(c, d).wait_recv()
        span = pl.ds(place(src, c, 0), step_width)

        def wait_far(e, _, src=src, c=c):
            w_wait(e, src, c)
            return 0

        lax.fori_loop(0, experts, wait_far, 0)
        if not last:
            def far(e, _, span=span):
                acc[e] += jnp.dot(xg[:, span], wv[e, span, :],
                                  preferred_element_type=jnp.float32)
                return 0

            lax.fori_loop(0, experts, far, 0)
            if i + 2 == len(forwards):
                forward(len(forwards))

    def pair_copy(j):
        return pltpu.make_async_remote_copy(
            src_ref=part.at[j * 2 + 1 - core], dst_ref=rxd.at[j],
            send_sem=ps_sem.at[j], recv_sem=pr_sem.at[j],
            device_id={"expert": other}, device_id_type=MESH)

    def sum_copy(d):
        return pltpu.make_async_remote_copy(
            src_ref=txx.at[d - 1], dst_ref=rxx.at[d - 1],
            send_sem=qs_sem.at[d - 1], recv_sem=qr_sem.at[d - 1],
            device_id={"expert": lax.rem(chip + d, chips) * 2 + core}, device_id_type=MESH)

    c, d = forwards[-1]
    span = pl.ds(place(lax.rem(chip - d + chips, chips), c, 0), step_width)
    band = 2 * owned
    rt = 64
    for d in list(range(1, chips)) + [0]:
        j = lax.rem(chip + d, chips)
        cols = pl.ds(pl.multiple_of(j * band, 128), band)
        for e in range(experts):
            acc[e, :, cols] += jnp.dot(xg[:, span], wv[e, span, cols],
                                       preferred_element_type=jnp.float32)

        def finish(r, _, cols=cols, j=j):
            at = pl.ds(pl.multiple_of(r * rt, rt), rt)
            total = jnp.zeros((rt, band), jnp.float32)
            for e in range(experts):
                half = acc[e, at, cols] * 0.5
                total = total + (half * jnp.tanh(half) + half) * gsc[e, at, :]
            total = total.astype(jnp.bfloat16)
            part[j * 2, at, :] = total[:, :owned]
            part[j * 2 + 1, at, :] = total[:, owned:]
            return 0

        lax.fori_loop(0, rows // rt, finish, 0)
        pair_copy(j).start()

    for d in range(1, chips):
        j = lax.rem(chip + d, chips)
        pair_copy(j).wait_recv()
        txx[d - 1] = (part[j * 2 + core].astype(jnp.float32)
                      + rxd[j].astype(jnp.float32)).astype(jnp.bfloat16)
        sum_copy(d).start()
    pair_copy(chip).wait_recv()
    total = part[chip * 2 + core].astype(jnp.float32) + rxd[chip].astype(jnp.float32)
    for d in range(1, chips):
        sum_copy(d).wait_recv()
        total = total + rxx[d - 1].astype(jnp.float32)
    comb[...] = total.astype(jnp.bfloat16)

    for c in range(chunks):
        out_copy(c).wait()
        side_copy(c).wait_send()
        for d in range(1, chips):
            cross_copy(c, d).wait_send()
            pass_copy(c, d).wait_send()
    for j in range(chips):
        pair_copy(j).wait_send()
    for d in range(1, chips):
        sum_copy(d).wait_send()


def att_chunks(width):
    return width // (2 * HEAD_DIM)


def shards(dp_size, group, queries, key_states, value_states, doc_lengths, move_plan,
           expert_ids, gate_weights, expert_weight):
    rows, width = queries.shape
    experts, depth, ff = expert_weight.shape
    chips = group // 2
    chunks = att_chunks(width)
    owned = ff // group
    bf16, f32 = jnp.bfloat16, jnp.float32
    hbm = pl.BlockSpec(memory_space=pl.ANY)
    smem = pl.BlockSpec(memory_space=pltpu.SMEM)
    vmem = pl.BlockSpec(memory_space=pltpu.VMEM)
    dma = pltpu.SemaphoreType.DMA
    return pl.pallas_call(
        functools.partial(kernel, dp_size, group),
        out_shape=(
            jax.ShapeDtypeStruct((rows, width), bf16),
            jax.ShapeDtypeStruct((rows, owned), bf16),
            jax.ShapeDtypeStruct((1,), f32),
        ),
        in_specs=[hbm, hbm, hbm, smem, smem, vmem, vmem, hbm],
        out_specs=(hbm, vmem, smem),
        scratch_shapes=[
            pltpu.VMEM((rows, width), bf16),
            pltpu.VMEM((rows, width), bf16),
            pltpu.VMEM((rows, width), bf16),
            pltpu.VMEM((experts, depth, ff), bf16),
            pltpu.VMEM((rows, depth), bf16),
            pltpu.VMEM((experts, rows, ff), f32),
            pltpu.VMEM((rows, rows), f32),
            pltpu.VMEM((experts, rows, 1), f32),
            pltpu.VMEM((group, rows, owned), bf16),
            pltpu.VMEM((chips, rows, owned), bf16),
            pltpu.VMEM((chips - 1, rows, owned), bf16),
            pltpu.VMEM((chips - 1, rows, owned), bf16),
            dma((3, chunks)),
            dma((experts, chips, chunks, 2)),
            dma((chunks,)),
            dma((chips - 1, chunks)),
            dma((chips - 1, chunks)),
            dma((chunks,)),
            dma((chunks,)),
            dma((chips - 1, chunks)),
            dma((chips - 1, chunks)),
            dma((chips,)),
            dma((chips,)),
            dma((chips - 1,)),
            dma((chips - 1,)),
        ],
        compiler_params=pltpu.CompilerParams(
            collective_id=0, has_side_effects=True, vmem_limit_bytes=66_000_000),
    )(queries, key_states, value_states, doc_lengths, move_plan, expert_ids, gate_weights,
      expert_weight)


def solution(mesh):
    in_specs = (
        P("dp", "expert"),
        P("dp", "expert"),
        P("dp", "expert"),
        P(),
        P(),
        P("dp", None),
        P("dp", None),
        P("expert", None, None),
    )
    out_specs = (P("dp", "expert"), P("dp", "expert"), P("dp"))
    body = functools.partial(shards, mesh.shape["dp"], mesh.shape["expert"])
    return jax.shard_map(body, mesh=mesh, in_specs=in_specs, out_specs=out_specs, check_vma=False)
```

time: 179 us -> 57.1 us (0.32)
  waiting for transfers between devices: 58.7 us -> 0 us
  Pallas kernels: 0 us -> 45.9 us
  matrix products: 39.8 us -> 0 us
  local copies, waits for them, and re-layouts: 44.9 us -> 8.38 us
  between operations: 22.6 us -> 2.45 us
  other arithmetic: 7.99 us -> 0 us
  starting transfers between devices: 4.13 us -> 0 us
    pallas_call x0 -> x1, Pallas kernels: none -> 45.9 us  [shards(): pl.pallas_call(functools.partial(kernel, dp_size, group), out_shape=(jax....]
    dot_general x10 -> x0, matrix products: 36.1 us -> none  [the longest x1 21.3 us: shards(): jnp.einsum('ecf,efg->ecg', picked, expert_weight, preferred_element_type=...]
    all_gather x1 -> x0, waiting for transfers between devices: 32.1 us -> none  [shards(): piece = lax.all_gather(attended, 'expert', axis=1, tiled=True)]
    all_to_all x1 -> x0, waiting for transfers between devices: 26.6 us -> none  [shards(): lax.all_to_all(activated, 'expert', split_axis=3, concat_axis=0, tiled=True)]
    gather x1 -> x0, local copies, waits for them, and re-layouts: 25 us -> none  [shards(): picked = extended[chosen_rows].reshape(local_experts, CAP, piece.shape[1])]
    unnamed x22 -> x5, local copies, waits for them, and re-layouts: 2.83 us -> 8.38 us
    concatenate x1 -> x0, local copies, waits for them, and re-layouts: 4.7 us -> none  [shards(): jnp.concatenate([piece, jnp.zeros((1, piece.shape[1]), piece.dtype)], 0)]
    all_to_all x1 -> x0, starting transfers between devices: 4.09 us -> none  [shards(): lax.all_to_all(activated, 'expert', split_axis=3, concat_axis=0, tiled=True)]
  transfers between devices with their start and end apart: 2 -> 0, of which waited for: 2 -> 0; matrix products, arithmetic and copies ran while one was open for 5% -> 0% of each run, Pallas kernels for 0% -> 0%
where the time goes in v1:
time: 57.1 us; the launch traced here: 56.7 us
  Pallas kernels  45.9 us (80%)
  local copies, waits for them, and re-layouts  8.38 us (15%)
  between operations  2.45 us (4%)
    pallas_call x1, Pallas kernels, shards(): pl.pallas_call(functools.partial(kernel, dp_size, group), out_shape=(jax....  45.9 us
    unnamed x5, local copies, waits for them, and re-layouts  8.38 us

profile of v1, /device:TPU:0, one launch (start us, length us, event | category | flops | bytes accessed | tf_op | source)
XLA Modules:
  0.0 56.7 jit_solution(5416840782936373799)
XLA Ops:
  0.6 1.3 %copy.11.plan = s32[8,2]{1,0:T(8,128)} copy(s32[8,2]{0,1:T(2,128)} %param.12) | data formatting | bytes 128 | tf_op args[4]
  2.0 1.6 %copy.12.ids = s32[512,8]{1,0:T(8,128)} copy(s32[512,8]{0,1:T(8,128)} %param.13) | data formatting | bytes 32768 | tf_op args[5]
  3.5 1.6 %copy.13.gates = f32[512,8]{1,0:T(8,128)} copy(f32[512,8]{0,1:T(8,128)} %param.14) | data formatting | bytes 32768 | tf_op args[6]
  5.1 45.9 %shard_map.103 = (bf16[512,1024]{1,0:T(8,128)(2,1)}, bf16[512,256]{1,0:T(8,128)(2,1)}, f32[1]{0:T(128)}) custom-call(bf16[512,1024]{1,0:T(8,128)(2,1)} %q_hbm.1, bf16[512,1024]{1,0:T(8,128)(2,1)} %k_hbm.1, bf16[512,1024]{1,0:T(8,128)(2,1)} %v_hbm.1, s32[8,8]{1,0:T(8,128)} %lens.1, s32[8,2]{1,0:T(8,128)} %copy.11.plan, s32[512,8]{1,0:T(8,128)} %copy.12.ids, ...), custom_call_target="tpu_custom_call" | custom-call | tf_op jit(solution)/shard_map/pallas_call | solution.py:311
  50.9 2.3 %copy.17 = bf16[512,1024]{1,0:T(8,128)(2,1)} copy(bf16[512,1024]{1,0:T(8,128)(2,1)} %get-tuple-element.6) | data formatting | bytes 2097152
  53.2 1.7 %copy.18 = bf16[512,256]{1,0:T(8,128)(2,1)} copy(bf16[512,256]{1,0:T(8,128)(2,1)} %get-tuple-element.7) | data formatting | bytes 524288

commit v2 on v1

--- a/solution.py
+++ b/solution.py
@@ -92,21 +92,7 @@
         return 0
 
     lax.fori_loop(0, experts * chunks, start_own, 0)
-    for d in range(1, chips):
-        def start_far(i, _, d=d):
-            w_start(lax.rem(i, experts), lax.rem(chip - d + chips, chips), i // experts)
-            return 0
-
-        lax.fori_loop(0, experts * chunks, start_far, 0)
-
-    partner = lax.rem(row + dp_size // 2, dp_size)
     docs = lens.shape[1]
-    own_total, own_moved = row_pairs(lens, row, plan[row, 1], docs, rows)
-    _, their_moved = row_pairs(lens, partner, plan[partner, 1], docs, rows)
-    work = own_total - jnp.where(plan[row, 0] != row, own_moved, 0)
-    work = work + jnp.where(plan[partner, 0] != partner, their_moved, 0)
-    load[0] = work.astype(jnp.float32) * (1.0 / (QBLOCK * QBLOCK))
-
     pos = lax.broadcasted_iota(jnp.int32, (rows, rows), 0)
     key_pos = lax.broadcasted_iota(jnp.int32, (rows, rows), 1)
     column = lax.broadcasted_iota(jnp.int32, (rows, 1), 0)
@@ -116,9 +102,6 @@
         edge = edge + lens[row, doc]
         starts = jnp.where(column >= edge, jnp.maximum(starts, edge), starts)
     bias[...] = jnp.where((key_pos <= pos) & (key_pos >= starts), 0.0, -1e30)
-    for e in range(experts):
-        chosen = ids[...] == me * experts + e
-        gsc[e] = jnp.sum(jnp.where(chosen, gates[...], 0.0), axis=1, keepdims=True)
 
     pl.semaphore_wait(barrier, chips)
 
@@ -177,6 +160,26 @@
 
     lax.fori_loop(0, chunks, attend, 0)
 
+    for d in range(1, chips):
+        def start_far(i, _, d=d):
+            w_start(lax.rem(i, experts), lax.rem(chip - d + chips, chips), i // experts)
+            return 0
+
+        lax.fori_loop(0, experts * chunks, start_far, 0)
+
+    partner = lax.rem(row + dp_size // 2, dp_size)
+    own_total, own_moved = row_pairs(lens, row, plan[1, row], docs, rows)
+    _, their_moved = row_pairs(lens, partner, plan[1, partner], docs, rows)
+    work = own_total - jnp.where(plan[0, row] != row, own_moved, 0)
+    work = work + jnp.where(plan[0, partner] != partner, their_moved, 0)
+    load[0] = work.astype(jnp.float32) * (1.0 / (QBLOCK * QBLOCK))
+
+    for e in range(experts):
+        chosen = ids[...] == me * experts + e
+        line = jnp.sum(jnp.where(chosen, gates[...], 0.0), axis=0, keepdims=True)
+        for r in range(0, rows, 128):
+            gsc[e, r:r + 128, :] = jnp.broadcast_to(line[:, r:r + 128], (128, 128)).T
+
     forwards = [(c, d) for c in range(chunks) for d in range(1, chips)]
     sent = [0]
 
@@ -258,7 +261,8 @@
             total = jnp.zeros((rt, band), jnp.float32)
             for e in range(experts):
                 half = acc[e, at, cols] * 0.5
-                total = total + (half * jnp.tanh(half) + half) * gsc[e, at, :]
+                total = total + (half * jnp.tanh(half) + half) * jnp.concatenate(
+                    [gsc[e, at, :]] * (band // 128), axis=1)
             total = total.astype(jnp.bfloat16)
             part[j * 2, at, :] = total[:, :owned]
             part[j * 2 + 1, at, :] = total[:, owned:]
@@ -325,7 +329,7 @@
             pltpu.VMEM((rows, depth), bf16),
             pltpu.VMEM((experts, rows, ff), f32),
             pltpu.VMEM((rows, rows), f32),
-            pltpu.VMEM((experts, rows, 1), f32),
+            pltpu.VMEM((experts, rows, 128), f32),
             pltpu.VMEM((group, rows, owned), bf16),
             pltpu.VMEM((chips, rows, owned), bf16),
             pltpu.VMEM((chips - 1, rows, owned), bf16),
@@ -346,8 +350,8 @@
         ],
         compiler_params=pltpu.CompilerParams(
             collective_id=0, has_side_effects=True, vmem_limit_bytes=66_000_000),
-    )(queries, key_states, value_states, doc_lengths, move_plan, expert_ids, gate_weights,
-      expert_weight)
+    )(queries, key_states, value_states, doc_lengths, move_plan.T, expert_ids.T,
+      gate_weights.T, expert_weight)
 
 
 def solution(mesh):

time: 57.1 us -> 51.4 us (0.900)
  local copies, waits for them, and re-layouts: 8.38 us -> 3.93 us
  Pallas kernels: 45.9 us -> 44.8 us
    unnamed x5 -> x2, local copies, waits for them, and re-layouts: 8.38 us -> 3.93 us
    pallas_call x1, Pallas kernels: 45.9 us -> 44.8 us  [shards(): pl.pallas_call(functools.partial(kernel, dp_size, group), out_shape=(jax....]
where the time goes in v2:
time: 51.4 us; the launch traced here: 51.1 us
  Pallas kernels  44.8 us (87%)
  local copies, waits for them, and re-layouts  3.93 us (8%)
  between operations  2.4 us (5%)
    pallas_call x1, Pallas kernels, shards(): pl.pallas_call(functools.partial(kernel, dp_size, group), out_shape=(jax....  44.8 us
    unnamed x2, local copies, waits for them, and re-layouts  3.93 us

profile of v2, /device:TPU:0, one launch (start us, length us, event | category | flops | bytes accessed | tf_op | source)
XLA Modules:
  0.0 51.1 jit_solution(13527025247540151024)
XLA Ops:
  0.6 44.8 %shard_map.103 = (bf16[512,1024]{1,0:T(8,128)(2,1)}, bf16[512,256]{1,0:T(8,128)(2,1)}, f32[1]{0:T(128)}) custom-call(bf16[512,1024]{1,0:T(8,128)(2,1)} %q_hbm.1, bf16[512,1024]{1,0:T(8,128)(2,1)} %k_hbm.1, bf16[512,1024]{1,0:T(8,128)(2,1)} %v_hbm.1, s32[8,8]{1,0:T(8,128)} %lens.1, s32[2,8]{1,0:T(2,128)} %bitcast.5, s32[8,512]{1,0:T(8,128)} %bitcast.3, ...), custom_call_target="tpu_custom_call" | custom-call | tf_op jit(solution)/shard_map/pallas_call | solution.py:315
  45.4 2.3 %copy.14 = bf16[512,1024]{1,0:T(8,128)(2,1)} copy(bf16[512,1024]{1,0:T(8,128)(2,1)} %get-tuple-element.6) | data formatting | bytes 2097152
  47.7 1.7 %copy.15 = bf16[512,256]{1,0:T(8,128)(2,1)} copy(bf16[512,256]{1,0:T(8,128)(2,1)} %get-tuple-element.7) | data formatting | bytes 524288

commit v3 on v2

--- a/solution.py
+++ b/solution.py
@@ -105,25 +105,30 @@
 
     pl.semaphore_wait(barrier, chips)
 
-    def cross_copy(c, d):
-        cols = pl.ds(place(chip, c, core), ck)
+    half = rows // 2
+
+    def band_of(b):
+        return pl.ds(b * half, half)
+
+    def cross_copy(b, c, d):
+        at = xg.at[band_of(b), pl.ds(place(chip, c, core), ck)]
         return pltpu.make_async_remote_copy(
-            src_ref=xg.at[:, cols], dst_ref=xg.at[:, cols],
-            send_sem=sx_sem.at[d - 1, c], recv_sem=rx_sem.at[d - 1, c],
+            src_ref=at, dst_ref=at,
+            send_sem=sx_sem.at[d - 1, b, c], recv_sem=rx_sem.at[d - 1, b, c],
             device_id={"expert": lax.rem(chip + d, chips) * 2 + core}, device_id_type=MESH)
 
-    def side_copy(c):
-        cols = pl.ds(place(chip, c, core), ck)
+    def side_copy(b, c):
+        at = xg.at[band_of(b), pl.ds(place(chip, c, core), ck)]
         return pltpu.make_async_remote_copy(
-            src_ref=xg.at[:, cols], dst_ref=xg.at[:, cols],
-            send_sem=sd_sem.at[c], recv_sem=rd_sem.at[c],
+            src_ref=at, dst_ref=at,
+            send_sem=sd_sem.at[b, c], recv_sem=rd_sem.at[b, c],
             device_id={"expert": other}, device_id_type=MESH)
 
-    def pass_copy(c, d):
-        cols = pl.ds(place(lax.rem(chip - d + chips, chips), c, core), ck)
+    def pass_copy(b, c, d):
+        at = xg.at[band_of(b), pl.ds(place(lax.rem(chip - d + chips, chips), c, core), ck)]
         return pltpu.make_async_remote_copy(
-            src_ref=xg.at[:, cols], dst_ref=xg.at[:, cols],
-            send_sem=sf_sem.at[d - 1, c], recv_sem=rf_sem.at[d - 1, c],
+            src_ref=at, dst_ref=at,
+            send_sem=sf_sem.at[d - 1, b, c], recv_sem=rf_sem.at[d - 1, b, c],
             device_id={"expert": other}, device_id_type=MESH)
 
     def out_copy(c):
@@ -132,16 +137,17 @@
             att_hbm.at[:, pl.ds(pl.multiple_of(c * ck, 128), ck)], out_sem.at[c])
 
     scale = HEAD_DIM ** -0.5 * LOG2E
-    qb = rows // 2
-
-    def attend(c, _):
-        for copy in in_copies(c):
-            copy.wait()
-        for h in range(ck // HEAD_DIM):
-            cols = pl.ds(pl.multiple_of(c * ck + h * HEAD_DIM, 128), HEAD_DIM)
-            dst = pl.ds(pl.multiple_of(place(chip, c, core) + h * HEAD_DIM, 128), HEAD_DIM)
-            for b in range(2):
-                low, high = b * qb, (b + 1) * qb
+
+    for b in range(2):
+        low, high = b * half, (b + 1) * half
+
+        def attend(c, _, b=b, low=low, high=high):
+            if b == 0:
+                for copy in in_copies(c):
+                    copy.wait()
+            for h in range(ck // HEAD_DIM):
+                cols = pl.ds(pl.multiple_of(c * ck + h * HEAD_DIM, 128), HEAD_DIM)
+                dst = pl.ds(pl.multiple_of(place(chip, c, core) + h * HEAD_DIM, 128), HEAD_DIM)
                 s = lax.dot_general(
                     qv[low:high, cols], kv[:high, cols], (((1,), (1,)), ((), ())),
                     preferred_element_type=jnp.float32)
@@ -152,13 +158,14 @@
                 o = jnp.dot(p.astype(jnp.bfloat16), vv[:high, cols],
                             preferred_element_type=jnp.float32)
                 xg[low:high, dst] = (o / norm).astype(jnp.bfloat16)
-        for d in range(1, chips):
-            cross_copy(c, d).start()
-        side_copy(c).start()
-        out_copy(c).start()
-        return 0
-
-    lax.fori_loop(0, chunks, attend, 0)
+            for d in range(1, chips):
+                cross_copy(b, c, d).start()
+            side_copy(b, c).start()
+            if b == 1:
+                out_copy(c).start()
+            return 0
+
+        lax.fori_loop(0, chunks, attend, 0)
 
     for d in range(1, chips):
         def start_far(i, _, d=d):
@@ -180,18 +187,21 @@
         for r in range(0, rows, 128):
             gsc[e, r:r + 128, :] = jnp.broadcast_to(line[:, r:r + 128], (128, 128)).T
 
-    forwards = [(c, d) for c in range(chunks) for d in range(1, chips)]
+    forwards = [(b, c, d) for b in range(2) for c in range(chunks) for d in range(1, chips)]
+    per_half = len(forwards) // 2
     sent = [0]
 
     def forward(count):
         while sent[0] < min(count, len(forwards)):
-            c, d = forwards[sent[0]]
-            cross_copy(c, d).wait_recv()
-            pass_copy(c, d).start()
+            b, c, d = forwards[sent[0]]
+            cross_copy(b, c, d).wait_recv()
+            pass_copy(b, c, d).start()
             sent[0] += 1
 
-    for c in range(chunks):
-        side_copy(c).wait_recv()
+    forward(1)
+    for b in range(2):
+        for c in range(chunks):
+            side_copy(b, c).wait_recv()
     own = pl.ds(pl.multiple_of(chip * chip_width, 128), chip_width)
     tile = ff // 2
     for e in range(experts):
@@ -208,92 +218,123 @@
             return 0
 
         lax.fori_loop(0, 2, near, 0)
-        if e == 0 or e == experts - 2:
-            forward(sent[0] + 1)
-
-    for i, (c, d) in enumerate(forwards):
-        last = i == len(forwards) - 1
-        forward(i + 2 if i + 2 < len(forwards) else i + 1)
-        src = lax.rem(chip - d + chips, chips)
-        pass_copy(c, d).wait_recv()
-        span = pl.ds(place(src, c, 0), step_width)
-
-        def wait_far(e, _, src=src, c=c):
-            w_wait(e, src, c)
-            return 0
-
-        lax.fori_loop(0, experts, wait_far, 0)
-        if not last:
-            def far(e, _, span=span):
-                acc[e] += jnp.dot(xg[:, span], wv[e, span, :],
-                                  preferred_element_type=jnp.float32)
+        forward(min(sent[0] + 1, per_half))
+
+    def pair_copy(b, j):
+        return pltpu.make_async_remote_copy(
+            src_ref=part.at[j * 2 + 1 - core, band_of(b)], dst_ref=rxd.at[j, band_of(b)],
+            send_sem=ps_sem.at[b, j], recv_sem=pr_sem.at[b, j],
+            device_id={"expert": other}, device_id_type=MESH)
+
+    def sum_copy(b, d):
+        return pltpu.make_async_remote_copy(
+            src_ref=txx.at[d - 1, band_of(b)], dst_ref=rxx.at[d - 1, band_of(b)],
+            send_sem=qs_sem.at[b, d - 1], recv_sem=qr_sem.at[b, d - 1],
+            device_id={"expert": lax.rem(chip + d, chips) * 2 + core}, device_id_type=MESH)
+
+    def exchange(b):
+        at = band_of(b)
+        for d in range(1, chips):
+            j = lax.rem(chip + d, chips)
+            pair_copy(b, j).wait_recv()
+            txx[d - 1, at, :] = (part[j * 2 + core, at, :].astype(jnp.float32)
+                                 + rxd[j, at, :].astype(jnp.float32)).astype(jnp.bfloat16)
+            sum_copy(b, d).start()
+
+    def arrive(b, c0, c1, d):
+        for c in range(c0, c1):
+            forward(forwards.index((b, c, d)) + 1)
+        for c in range(c0, c1):
+            pass_copy(b, c, d).wait_recv()
+            if b == 0:
+                def wait_far(e, _, c=c, d=d):
+                    w_wait(e, lax.rem(chip - d + chips, chips), c)
+                    return 0
+
+                lax.fori_loop(0, experts, wait_far, 0)
+        return pl.ds(place(lax.rem(chip - d + chips, chips), c0, 0), (c1 - c0) * step_width)
+
+    columns = 2 * owned
+    rt = 64
+
+    def add_far(b, e, span, cols):
+        at = band_of(b)
+        acc[e, at, cols] += jnp.dot(xg[at, span], wv[e, span, cols],
+                                    preferred_element_type=jnp.float32)
+
+    def close(b, span):
+        for d in list(range(1, chips)) + [0]:
+            j = lax.rem(chip + d, chips)
+            cols = pl.ds(pl.multiple_of(j * columns, 128), columns)
+            for e in range(experts):
+                add_far(b, e, span, cols)
+
+            def finish(r, _, cols=cols, j=j):
+                at = pl.ds(pl.multiple_of(b * half + r * rt, rt), rt)
+                total = jnp.zeros((rt, columns), jnp.float32)
+                for e in range(experts):
+                    h = acc[e, at, cols] * 0.5
+                    total = total + (h * jnp.tanh(h) + h) * jnp.concatenate(
+                        [gsc[e, at, :]] * (columns // 128), axis=1)
+                total = total.astype(jnp.bfloat16)
+                part[j * 2, at, :] = total[:, :owned]
+                part[j * 2 + 1, at, :] = total[:, owned:]
                 return 0
 
-            lax.fori_loop(0, experts, far, 0)
-            if i + 2 == len(forwards):
-                forward(len(forwards))
-
-    def pair_copy(j):
-        return pltpu.make_async_remote_copy(
-            src_ref=part.at[j * 2 + 1 - core], dst_ref=rxd.at[j],
-            send_sem=ps_sem.at[j], recv_sem=pr_sem.at[j],
-            device_id={"expert": other}, device_id_type=MESH)
-
-    def sum_copy(d):
-        return pltpu.make_async_remote_copy(
-            src_ref=txx.at[d - 1], dst_ref=rxx.at[d - 1],
-            send_sem=qs_sem.at[d - 1], recv_sem=qr_sem.at[d - 1],
-            device_id={"expert": lax.rem(chip + d, chips) * 2 + core}, device_id_type=MESH)
-
-    c, d = forwards[-1]
-    span = pl.ds(place(lax.rem(chip - d + chips, chips), c, 0), step_width)
-    band = 2 * owned
-    rt = 64
-    for d in list(range(1, chips)) + [0]:
-        j = lax.rem(chip + d, chips)
-        cols = pl.ds(pl.multiple_of(j * band, 128), band)
-        for e in range(experts):
-            acc[e, :, cols] += jnp.dot(xg[:, span], wv[e, span, cols],
-                                       preferred_element_type=jnp.float32)
-
-        def finish(r, _, cols=cols, j=j):
-            at = pl.ds(pl.multiple_of(r * rt, rt), rt)
-            total = jnp.zeros((rt, band), jnp.float32)
+            lax.fori_loop(0, half // rt, finish, 0)
+            pair_copy(b, j).start()
+
+    whole = pl.ds(0, ff)
+    for d in range(1, chips):
+        span = arrive(0, 0, chunks, d)
+        if d < chips - 1:
             for e in range(experts):
-                half = acc[e, at, cols] * 0.5
-                total = total + (half * jnp.tanh(half) + half) * jnp.concatenate(
-                    [gsc[e, at, :]] * (band // 128), axis=1)
-            total = total.astype(jnp.bfloat16)
-            part[j * 2, at, :] = total[:, :owned]
-            part[j * 2 + 1, at, :] = total[:, owned:]
-            return 0
-
-        lax.fori_loop(0, rows // rt, finish, 0)
-        pair_copy(j).start()
-
+                add_far(0, e, span, whole)
+    forward(per_half + 1)
+    close(0, span)
+    forward(per_half + 2)
+    exchanged = False
+    if chunks > 1:
+        for d in range(1, chips):
+            span = arrive(1, 0, chunks - 1, d)
+            for e in range(experts):
+                add_far(1, e, span, whole)
+                if e == 0 and not exchanged:
+                    exchange(0)
+                    exchanged = True
+                if d == chips - 1 and e == experts // 2:
+                    forward(len(forwards))
+    if not exchanged:
+        exchange(0)
     for d in range(1, chips):
-        j = lax.rem(chip + d, chips)
-        pair_copy(j).wait_recv()
-        txx[d - 1] = (part[j * 2 + core].astype(jnp.float32)
-                      + rxd[j].astype(jnp.float32)).astype(jnp.bfloat16)
-        sum_copy(d).start()
-    pair_copy(chip).wait_recv()
-    total = part[chip * 2 + core].astype(jnp.float32) + rxd[chip].astype(jnp.float32)
-    for d in range(1, chips):
-        sum_copy(d).wait_recv()
-        total = total + rxx[d - 1].astype(jnp.float32)
-    comb[...] = total.astype(jnp.bfloat16)
+        span = arrive(1, chunks - 1, chunks, d)
+        if d < chips - 1:
+            for e in range(experts):
+                add_far(1, e, span, whole)
+    close(1, span)
+    exchange(1)
+    for b in range(2):
+        at = band_of(b)
+        pair_copy(b, chip).wait_recv()
+        total = (part[chip * 2 + core, at, :].astype(jnp.float32)
+                 + rxd[chip, at, :].astype(jnp.float32))
+        for d in range(1, chips):
+            sum_copy(b, d).wait_recv()
+            total = total + rxx[d - 1, at, :].astype(jnp.float32)
+        comb[at, :] = total.astype(jnp.bfloat16)
 
     for c in range(chunks):
         out_copy(c).wait()
-        side_copy(c).wait_send()
+        for b in range(2):
+            side_copy(b, c).wait_send()
+            for d in range(1, chips):
+                cross_copy(b, c, d).wait_send()
+                pass_copy(b, c, d).wait_send()
+    for b in range(2):
+        for j in range(chips):
+            pair_copy(b, j).wait_send()
         for d in range(1, chips):
-            cross_copy(c, d).wait_send()
-            pass_copy(c, d).wait_send()
-    for j in range(chips):
-        pair_copy(j).wait_send()
-    for d in range(1, chips):
-        sum_copy(d).wait_send()
+            sum_copy(b, d).wait_send()
 
 
 def att_chunks(width):
@@ -337,16 +378,16 @@
             dma((3, chunks)),
             dma((experts, chips, chunks, 2)),
             dma((chunks,)),
-            dma((chips - 1, chunks)),
-            dma((chips - 1, chunks)),
-            dma((chunks,)),
-            dma((chunks,)),
-            dma((chips - 1, chunks)),
-            dma((chips - 1, chunks)),
-            dma((chips,)),
-            dma((chips,)),
-            dma((chips - 1,)),
-            dma((chips - 1,)),
+            dma((chips - 1, 2, chunks)),
+            dma((chips - 1, 2, chunks)),
+            dma((2, chunks)),
+            dma((2, chunks)),
+            dma((chips - 1, 2, chunks)),
+            dma((chips - 1, 2, chunks)),
+            dma((2, chips)),
+            dma((2, chips)),
+            dma((2, chips - 1)),
+            dma((2, chips - 1)),
         ],
         compiler_params=pltpu.CompilerParams(
             collective_id=0, has_side_effects=True, vmem_limit_bytes=66_000_000),

time: 51.4 us -> 48.3 us (0.940)
  Pallas kernels: 44.8 us -> 41.7 us
    pallas_call x1, Pallas kernels: 44.8 us -> 41.7 us  [shards(): pl.pallas_call(functools.partial(kernel, dp_size, group), out_shape=(jax....]
where the time goes in v3:
time: 48.3 us; the launch traced here: 48 us
  Pallas kernels  41.7 us (86%)
  local copies, waits for them, and re-layouts  3.93 us (8%)
  between operations  2.4 us (5%)
    pallas_call x1, Pallas kernels, shards(): pl.pallas_call(functools.partial(kernel, dp_size, group), out_shape=(jax....  41.7 us
    unnamed x2, local copies, waits for them, and re-layouts  3.93 us

profile of v3, /device:TPU:0, one launch (start us, length us, event | category | flops | bytes accessed | tf_op | source)
XLA Modules:
  0.0 48.0 jit_solution(4665574342723903651)
XLA Ops:
  0.6 41.7 %shard_map.103 = (bf16[512,1024]{1,0:T(8,128)(2,1)}, bf16[512,256]{1,0:T(8,128)(2,1)}, f32[1]{0:T(128)}) custom-call(bf16[512,1024]{1,0:T(8,128)(2,1)} %q_hbm.1, bf16[512,1024]{1,0:T(8,128)(2,1)} %k_hbm.1, bf16[512,1024]{1,0:T(8,128)(2,1)} %v_hbm.1, s32[8,8]{1,0:T(8,128)} %lens.1, s32[2,8]{1,0:T(2,128)} %bitcast.5, s32[8,512]{1,0:T(8,128)} %bitcast.3, ...), custom_call_target="tpu_custom_call" | custom-call | tf_op jit(solution)/shard_map/pallas_call | solution.py:356
  42.3 2.3 %copy.14 = bf16[512,1024]{1,0:T(8,128)(2,1)} copy(bf16[512,1024]{1,0:T(8,128)(2,1)} %get-tuple-element.6) | data formatting | bytes 2097152
  44.6 1.7 %copy.15 = bf16[512,256]{1,0:T(8,128)(2,1)} copy(bf16[512,256]{1,0:T(8,128)(2,1)} %get-tuple-element.7) | data formatting | bytes 524288

commit v4 on v3

--- a/solution.py
+++ b/solution.py
@@ -91,17 +91,13 @@
         w_start(i // chunks, chip, lax.rem(i, chunks))
         return 0
 
-    lax.fori_loop(0, experts * chunks, start_own, 0)
     docs = lens.shape[1]
-    pos = lax.broadcasted_iota(jnp.int32, (rows, rows), 0)
-    key_pos = lax.broadcasted_iota(jnp.int32, (rows, rows), 1)
     column = lax.broadcasted_iota(jnp.int32, (rows, 1), 0)
     starts = jnp.zeros((rows, 1), jnp.int32)
     edge = jnp.int32(0)
     for doc in range(docs):
         edge = edge + lens[row, doc]
         starts = jnp.where(column >= edge, jnp.maximum(starts, edge), starts)
-    bias[...] = jnp.where((key_pos <= pos) & (key_pos >= starts), 0.0, -1e30)
 
     pl.semaphore_wait(barrier, chips)
 
@@ -140,6 +136,10 @@
 
     for b in range(2):
         low, high = b * half, (b + 1) * half
+        pos = lax.broadcasted_iota(jnp.int32, (half, high), 0) + low
+        key_pos = lax.broadcasted_iota(jnp.int32, (half, high), 1)
+        bias[low:high, :high] = jnp.where(
+            (key_pos <= pos) & (key_pos >= starts[low:high]), 0.0, -1e30)
 
         def attend(c, _, b=b, low=low, high=high):
             if b == 0:
@@ -166,6 +166,8 @@
             return 0
 
         lax.fori_loop(0, chunks, attend, 0)
+        if b == 0:
+            lax.fori_loop(0, experts * chunks, start_own, 0)
 
     for d in range(1, chips):
         def start_far(i, _, d=d):

time: 48.3 us -> 48.7 us (level)
  no operation moved by 1% of the time
where the time goes in v4:
time: 48.7 us; the launch traced here: 48.4 us
  Pallas kernels  42.1 us (86%)
  local copies, waits for them, and re-layouts  3.93 us (8%)
  between operations  2.4 us (5%)
    pallas_call x1, Pallas kernels, shards(): pl.pallas_call(functools.partial(kernel, dp_size, group), out_shape=(jax....  42.1 us
    unnamed x2, local copies, waits for them, and re-layouts  3.93 us

profile of v4, /device:TPU:0, one launch (start us, length us, event | category | flops | bytes accessed | tf_op | source)
XLA Modules:
  0.0 48.4 jit_solution(17520460233827825044)
XLA Ops:
  0.6 42.1 %shard_map.103 = (bf16[512,1024]{1,0:T(8,128)(2,1)}, bf16[512,256]{1,0:T(8,128)(2,1)}, f32[1]{0:T(128)}) custom-call(bf16[512,1024]{1,0:T(8,128)(2,1)} %q_hbm.1, bf16[512,1024]{1,0:T(8,128)(2,1)} %k_hbm.1, bf16[512,1024]{1,0:T(8,128)(2,1)} %v_hbm.1, s32[8,8]{1,0:T(8,128)} %lens.1, s32[2,8]{1,0:T(2,128)} %bitcast.5, s32[8,512]{1,0:T(8,128)} %bitcast.3, ...), custom_call_target="tpu_custom_call" | custom-call | tf_op jit(solution)/shard_map/pallas_call | solution.py:358
  42.7 2.3 %copy.14 = bf16[512,1024]{1,0:T(8,128)(2,1)} copy(bf16[512,1024]{1,0:T(8,128)(2,1)} %get-tuple-element.6) | data formatting | bytes 2097152
  45.0 1.7 %copy.15 = bf16[512,256]{1,0:T(8,128)(2,1)} copy(bf16[512,256]{1,0:T(8,128)(2,1)} %get-tuple-element.7) | data formatting | bytes 524288
